TPU v7x, 32 devices: a whole 2x2x4 slice. The times are simulated.
32 devices in a mesh: blk: 8 (over z, x), lane: 4 (over y, core).
Axes of the slice: x: 2, y: 2, z: 4, core: 2. Of those that a mesh axis runs over, the one named last changes fastest.
Arguments:
- left_factor: bfloat16 [4096, 512], P('blk'), may hold values from -6 to 6
- right_factor: bfloat16 [4, 4096, 512], P('lane', 'blk'), may hold values from -6 to 6
- observed: bfloat16 [4, 4, 512, 4096], P('lane', None, None, 'blk'), may hold values from -6 to 6
- row_codes: int32 [4096], P('blk'), may hold values from 0 to 1073741823
- shift_codes: int32 [4, 4, 4096], P('lane', None, 'blk'), may hold values from 0 to 29
Outputs:
- left_out: bfloat16 [4096, 512], P('blk')
- right_out: bfloat16 [4, 4096, 512], P('lane', 'blk')
Inputs may be any that keep to these rules, and one draw needn't show every extreme that they name: `row_codes`: each row's word carries thirty independent sampling bits. `shift_codes`: A bit number for each lane, cycle step and visited tile entry column.
All inputs are finite; a program needn't handle non-finite values.
Results may differ from a plain program's by a relative error of at most 0.013.
Values may be sent and summed in bfloat16 or wider, within the bound.
A program may use at most 64 MiB of HBM per device.

v0:
```python
import math

import jax
import jax.numpy as jnp
from jax import lax
from jax.sharding import PartitionSpec as P

step_right = 0.25
step_left = 0.1


def passed_along(value, axis, steps):
    count = lax.axis_size(axis)
    pairs = [(source, (source + steps) % count) for source in range(count)]
    return lax.ppermute(value, axis, pairs)


def visit_tile(right_part, left_factor, target, row_codes, shifts, root_scale):
    predicted = (
        lax.dot_general(
            right_part, left_factor, (((1,), (1,)), ((), ())), preferred_element_type=jnp.float32
        )
        * root_scale
    )
    sample_bits = jnp.right_shift(row_codes[None, :], shifts[:, None]) & 1
    error_tile = jnp.where(sample_bits == 1, predicted - target.astype(jnp.float32), 0.0).astype(
        jnp.bfloat16
    )
    grad_right = jnp.dot(error_tile, left_factor, preferred_element_type=jnp.float32)
    grad_left = lax.dot_general(
        error_tile, right_part, (((0,), (0,)), ((), ())), preferred_element_type=jnp.float32
    )
    updated = (right_part.astype(jnp.float32) - step_right * root_scale * grad_right).astype(
        jnp.bfloat16
    )
    return (updated, grad_left)


def local(left_factor, right_factor, observed, row_codes, shift_codes):
    rank_size = left_factor.shape[1]
    root_scale = 1.0 / math.sqrt(rank_size)
    cycle_steps = observed.shape[1]
    column_count = observed.shape[2]
    right_now = right_factor[0]
    grad_sum = jnp.zeros(left_factor.shape, jnp.float32)
    for cycle_step in range(cycle_steps):
        target = observed[0, cycle_step]
        shifts = shift_codes[0, cycle_step]
        last_step = cycle_step + 1 == cycle_steps
        half_cols = column_count // 2
        pieces = []
        for portion in range(2):
            first_col = portion * half_cols
            updated, grad_left = visit_tile(
                right_now[first_col : first_col + half_cols],
                left_factor,
                target[first_col : first_col + half_cols],
                row_codes,
                shifts[first_col : first_col + half_cols],
                root_scale,
            )
            grad_sum = grad_sum + grad_left
            pieces.append(updated if last_step else passed_along(updated, "blk", 1))
        right_now = jnp.concatenate(pieces, axis=0)
    summed = lax.psum(grad_sum.astype(jnp.bfloat16), "lane").astype(jnp.float32)
    left_out = (left_factor.astype(jnp.float32) - step_left * root_scale * summed).astype(
        jnp.bfloat16
    )
    return (left_out, right_now[None])


def solution(mesh):
    in_specs = (
        P("blk", None),
        P("lane", "blk", None),
        P("lane", None, None, "blk"),
        P("blk"),
        P("lane", None, "blk"),
    )
    out_specs = (P("blk", None), P("lane", "blk", None))
    return jax.shard_map(local, mesh=mesh, in_specs=in_specs, out_specs=out_specs, check_vma=False)
```

profile of v0, /device:TPU:0, one launch (start us, length us, event | category | flops | bytes accessed | tf_op | source)
XLA Modules:
  0.0 94.1 jit_solution(8575521751137089536)
XLA Ops:
  7.2 0.0 copy-start
  7.2 0.0 copy-start.3
  7.2 0.0 copy-start.1
  7.2 0.0 all-reduce.2.cloned.1.call-start
  7.2 0.0 copy-start.2
  7.3 0.9 fusion.43
  8.2 1.6 %fusion.27 = bf16[256,512]{1,0:T(8,128)(2,1)S(1)} fusion(bf16[512,512]{1,0:T(8,128)(2,1)} %param.5, bf16[1,4,512,512]{3,2,1,0:T(8,128)(2,1)} %param.7, s32[256]{0:T(256)S(1)} %bitcast.97, s32[512]{0:T(512)} %param.8, bf16[1,512,512]{2,1,0:T(8,128)(2,1)} %param.6), kind=kOutput, calls=%fused_computation.45 | convolution fusion | flops 135266304 | bytes 1313792 | tf_op jit(solution)/shard_map/dot_general | solution.py:20
  9.8 0.0 copy-done
  9.8 0.0 copy-done.1
  9.8 0.3 fusion.25
  10.1 3.0 %collective-permute-start.1 = (bf16[256,512]{1,0:T(8,128)(2,1)S(1)}, bf16[256,512]{1,0:T(8,128)(2,1)S(1)}, u32[]{:S(2)}, u32[]{:S(2)}) collective-permute-start(bf16[256,512]{1,0:T(8,128)(2,1)S(1)} %fusion.25), channel_id=1, source_target_pairs={{0,4},{4,8},{8,12},{12,16},{16,20},{20,24},{24,28},{28,0},{1,5},{5... | collective-permute-start | bytes 786440 | tf_op jit(solution)/shard_map/ppermute | solution.py:15
  13.1 0.4 fusion.26
  13.5 0.3 fusion.24
  13.8 1.6 %collective-permute-start = (bf16[256,512]{1,0:T(8,128)(2,1)S(1)}, bf16[256,512]{1,0:T(8,128)(2,1)S(1)}, u32[]{:S(2)}, u32[]{:S(2)}) collective-permute-start(bf16[256,512]{1,0:T(8,128)(2,1)S(1)} %fusion.24), channel_id=1, source_target_pairs={{0,4},{4,8},{8,12},{12,16},{16,20},{20,24},{24,28},{28,0},{1,5},{5... | collective-permute-start | bytes 786440 | tf_op jit(solution)/shard_map/ppermute | solution.py:15
  15.4 0.3 fusion.36
  15.7 0.3 convolution_add_fusion.1
  16.1 7.2 %collective-permute-done.1 = bf16[256,512]{1,0:T(8,128)(2,1)S(1)} collective-permute-done((bf16[256,512]{1,0:T(8,128)(2,1)S(1)}, bf16[256,512]{1,0:T(8,128)(2,1)S(1)}, u32[]{:S(2)}, u32[]{:S(2)}) %collective-permute-start.1) | collective-permute-done | bytes 262176 | tf_op jit(solution)/shard_map/ppermute | solution.py:15
  23.3 0.4 fusion.29
  23.7 0.3 subtract_convert_fusion.5
  24.0 0.1 collective-permute-start.3
  24.1 4.3 %collective-permute-done = bf16[256,512]{1,0:T(8,128)(2,1)S(1)} collective-permute-done((bf16[256,512]{1,0:T(8,128)(2,1)S(1)}, bf16[256,512]{1,0:T(8,128)(2,1)S(1)}, u32[]{:S(2)}, u32[]{:S(2)}) %collective-permute-start) | collective-permute-done | bytes 262176 | tf_op jit(solution)/shard_map/ppermute | solution.py:15
  28.4 0.4 fusion.28
  28.8 0.3 subtract_convert_fusion.6
  29.1 0.1 collective-permute-start.2
  29.1 0.3 fusion.44
  29.5 4.5 %collective-permute-done.3 = bf16[256,512]{1,0:T(8,128)(2,1)S(1)} collective-permute-done((bf16[256,512]{1,0:T(8,128)(2,1)S(1)}, bf16[256,512]{1,0:T(8,128)(2,1)S(1)}, u32[]{:S(2)}, u32[]{:S(2)}) %collective-permute-start.3) | collective-permute-done | bytes 262176 | tf_op jit(solution)/shard_map/ppermute | solution.py:15
  34.0 0.4 fusion.31
  34.4 0.3 subtract_convert_fusion.3
  34.7 0.1 collective-permute-start.5
  34.8 6.2 %collective-permute-done.2 = bf16[256,512]{1,0:T(8,128)(2,1)S(1)} collective-permute-done((bf16[256,512]{1,0:T(8,128)(2,1)S(1)}, bf16[256,512]{1,0:T(8,128)(2,1)S(1)}, u32[]{:S(2)}, u32[]{:S(2)}) %collective-permute-start.2) | collective-permute-done | bytes 262176 | tf_op jit(solution)/shard_map/ppermute | solution.py:15
  41.0 0.4 fusion.30
  41.4 0.3 subtract_convert_fusion.4
  41.7 0.1 collective-permute-start.4
  41.8 0.3 fusion.45
  42.1 0.3 fusion.46
  42.4 8.4 %collective-permute-done.4 = bf16[256,512]{1,0:T(8,128)(2,1)S(1)} collective-permute-done((bf16[256,512]{1,0:T(8,128)(2,1)S(1)}, bf16[256,512]{1,0:T(8,128)(2,1)S(1)}, u32[]{:S(2)}, u32[]{:S(2)}) %collective-permute-start.4) | collective-permute-done | bytes 262176 | tf_op jit(solution)/shard_map/ppermute | solution.py:15
  50.8 0.4 fusion.32
  51.2 0.3 fusion.47
  51.5 0.0 collective-permute-done.5
  51.5 0.4 fusion.33
  51.9 0.3 fusion.48
  52.2 1.3 %fusion.5 = bf16[512,512]{1,0:T(8,128)(2,1)} fusion(f32[512,512]{1,0:T(8,128)S(1)} %fusion.48, f32[512,512]{1,0:T(8,128)S(1)} %fusion.47, f32[512,512]{1,0:T(8,128)S(1)} %fusion.46, f32[512,512]{1,0:T(8,128)S(1)} %fusion.45, f32[512,512]{1,0:T(8,128)S(1)} %fusion.44, f32[512,512]{1,0:T(8,128)S(1)} %convolution_add_fusion.1, ...), kind=kOutput, calls=%fused_computation.7 | convolution fusion | flops 136052736 | bytes 7340032 | tf_op jit(solution)/shard_map/dot_general | solution.py:30
  53.5 0.0 all-reduce.2.cloned.1.call-update
  53.5 0.3 subtract_convert_fusion.1
  53.9 0.3 subtract_convert_fusion.2
  54.2 0.8 maximum_bitcast_fusion
  55.0 30.3 %all-reduce.2.cloned.1.call-done = bf16[512,512]{1,0:T(8,128)(2,1)} async-done(((bf16[512,512]{1,0:T(8,128)(2,1)}), bf16[512,512]{1,0:T(8,128)(2,1)}) %all-reduce.2.cloned.1.call-update) | async-done | bytes 524304 | tf_op jit(solution)/shard_map/psum | solution.py:65
  85.3 2.0 %subtract_convert_fusion = bf16[512,512]{1,0:T(8,128)(2,1)} fusion(bf16[512,512]{1,0:T(8,128)(2,1)} %all-reduce.2.cloned.1.call-done, bf16[512,512]{1,0:T(8,128)(2,1)S(1)} %copy-done), kind=kLoop, calls=%fused_computation.52 | loop fusion | flops 1310720 | bytes 1572864 | tf_op jit(solution)/shard_map/convert_element_type | solution.py:66
  (2 shorter events, 0.0 us)
Async XLA Ops:
  7.2 2.6 %copy-start = (bf16[512,512]{1,0:T(8,128)(2,1)S(1)}, bf16[512,512]{1,0:T(8,128)(2,1)}, u32[]{:S(2)}) copy-start(bf16[512,512]{1,0:T(8,128)(2,1)} %param.5) | copy-start | bytes 1572868
  7.2 5.9 %copy-start.3 = (s32[512]{0:T(512)S(1)}, s32[512]{0:T(512)}, u32[]{:S(2)}) copy-start(s32[512]{0:T(512)} %param.8) | copy-start | bytes 6148
  7.2 2.6 %copy-start.1 = (bf16[1,512,512]{2,1,0:T(8,128)(2,1)S(1)}, bf16[1,512,512]{2,1,0:T(8,128)(2,1)}, u32[]{:S(2)}) copy-start(bf16[1,512,512]{2,1,0:T(8,128)(2,1)} %param.6) | copy-start | bytes 1572868
  7.2 78.1 %all-reduce.2.cloned.1.call-start = ((), (), s32[]{:S(2)}) async-start(), calls=%async_computation | async-start | bytes 1048576 | tf_op jit(solution)/shard_map/psum | solution.py:65
  7.2 5.9 %copy-start.2 = (bf16[1,4,512,512]{3,2,1,0:T(8,128)(2,1)S(1)}, bf16[1,4,512,512]{3,2,1,0:T(8,128)(2,1)}, u32[]{:S(2)}) copy-start(bf16[1,4,512,512]{3,2,1,0:T(8,128)(2,1)} %param.7) | copy-start | bytes 6291460
  10.1 13.2 %collective-permute-start.1 = (bf16[256,512]{1,0:T(8,128)(2,1)S(1)}, bf16[256,512]{1,0:T(8,128)(2,1)S(1)}, u32[]{:S(2)}, u32[]{:S(2)}) collective-permute-start(bf16[256,512]{1,0:T(8,128)(2,1)S(1)} %fusion.25), channel_id=1, source_target_pairs={{0,4},{4,8},{8,12},{12,16},{16,20},{20,24},{24,28},{28,0},{1,5},{5... | collective-permute-start | bytes 786440 | tf_op jit(solution)/shard_map/ppermute | solution.py:15
  13.8 14.6 %collective-permute-start = (bf16[256,512]{1,0:T(8,128)(2,1)S(1)}, bf16[256,512]{1,0:T(8,128)(2,1)S(1)}, u32[]{:S(2)}, u32[]{:S(2)}) collective-permute-start(bf16[256,512]{1,0:T(8,128)(2,1)S(1)} %fusion.24), channel_id=1, source_target_pairs={{0,4},{4,8},{8,12},{12,16},{16,20},{20,24},{24,28},{28,0},{1,5},{5... | collective-permute-start | bytes 786440 | tf_op jit(solution)/shard_map/ppermute | solution.py:15
  24.0 10.0 %collective-permute-start.3 = (bf16[256,512]{1,0:T(8,128)(2,1)S(1)}, bf16[256,512]{1,0:T(8,128)(2,1)S(1)}, u32[]{:S(2)}, u32[]{:S(2)}) collective-permute-start(bf16[256,512]{1,0:T(8,128)(2,1)S(1)} %subtract_convert_fusion.5), channel_id=1, source_target_pairs={{0,4},{4,8},{8,12},{12,16},{16,20},{20,24},{24,28},{28,0},{1,5},{5... | collective-permute-start | bytes 786440 | tf_op jit(solution)/shard_map/ppermute | solution.py:15
  29.1 11.9 %collective-permute-start.2 = (bf16[256,512]{1,0:T(8,128)(2,1)S(1)}, bf16[256,512]{1,0:T(8,128)(2,1)S(1)}, u32[]{:S(2)}, u32[]{:S(2)}) collective-permute-start(bf16[256,512]{1,0:T(8,128)(2,1)S(1)} %subtract_convert_fusion.6), channel_id=1, source_target_pairs={{0,4},{4,8},{8,12},{12,16},{16,20},{20,24},{24,28},{28,0},{1,5},{5... | collective-permute-start | bytes 786440 | tf_op jit(solution)/shard_map/ppermute | solution.py:15
  34.7 16.8 %collective-permute-start.5 = (bf16[256,512]{1,0:T(8,128)(2,1)S(1)}, bf16[256,512]{1,0:T(8,128)(2,1)S(1)}, u32[]{:S(2)}, u32[]{:S(2)}) collective-permute-start(bf16[256,512]{1,0:T(8,128)(2,1)S(1)} %subtract_convert_fusion.3), channel_id=1, source_target_pairs={{0,4},{4,8},{8,12},{12,16},{16,20},{20,24},{24,28},{28,0},{1,5},{5... | collective-permute-start | bytes 786440 | tf_op jit(solution)/shard_map/ppermute | solution.py:15
  41.7 9.1 %collective-permute-start.4 = (bf16[256,512]{1,0:T(8,128)(2,1)S(1)}, bf16[256,512]{1,0:T(8,128)(2,1)S(1)}, u32[]{:S(2)}, u32[]{:S(2)}) collective-permute-start(bf16[256,512]{1,0:T(8,128)(2,1)S(1)} %subtract_convert_fusion.4), channel_id=1, source_target_pairs={{0,4},{4,8},{8,12},{12,16},{16,20},{20,24},{24,28},{28,0},{1,5},{5... | collective-permute-start | bytes 786440 | tf_op jit(solution)/shard_map/ppermute | solution.py:15
Sparse Core Ops, SparseCore 0:
  53.7 31.5 all-reduce.1
where the time goes:
time: 94.3 us; the launch traced here: 94.1 us
  waiting for transfers between devices  61.1 us (65%)
  between operations  14.3 us (15%)
  matrix products  10.2 us (11%)
  starting transfers between devices  4.89 us (5%)
  other arithmetic  2.82 us (3%)
  local copies, waits for them, and re-layouts  0.95 us (1%)
    ppermute x6, waiting for transfers between devices, passed_along(): return lax.ppermute(value, axis, pairs)  30.7 us
    psum x1, waiting for transfers between devices, local(): summed = lax.psum(grad_sum.astype(jnp.bfloat16), 'lane').astype(jnp.float32)  30.3 us
    ppermute x6, starting transfers between devices, passed_along(): return lax.ppermute(value, axis, pairs)  4.85 us
    dot_general x8, matrix products, visit_tile(): lax.dot_general(right_part, left_factor, (((1,), (1,)), ((), ())), prefer...  4.16 us
    dot_general x8, matrix products, visit_tile(): lax.dot_general(error_tile, right_part, (((0,), (0,)), ((), ())), preferr...  3.58 us
    dot_general x8, matrix products, visit_tile(): jnp.dot(error_tile, left_factor, preferred_element_type=jnp.float32)  2.42 us
    convert_element_type x1, other arithmetic, local(): (left_factor.astype(jnp.float32) - step_left * root_scale * summed).astyp...  1.99 us
  transfers between devices with their start and end apart: 7, of which 6 were waited for; matrix products, arithmetic and copies ran while one was open for 8% of the time, Pallas kernels for 0%

commit v1 on v0

v1 whole, which is shorter than its diff:
```python
import functools
import math

import jax
import jax.numpy as jnp
from jax import lax
from jax.experimental import pallas as pl
from jax.experimental.pallas import tpu as pltpu
from jax.sharding import PartitionSpec as P

step_right = 0.25
step_left = 0.1

CHUNKS = 4
PIECES = 4
MESH = pl.DeviceIdType.MESH


def kernel(
    blocks, lanes,
    left_hbm, right_hbm, obs_hbm, codes_ref, shift_ref,
    left_out, right_out,
    left, visited, updated, obs, grad, pair_out, pair_in, peer_out, peer_in, result,
    load_sem, send_sem, recv_sem, store_sem, pair_send, pair_recv, peer_send, peer_recv, last_send, last_recv, out_sem,
):
    steps, cols, rows = obs.shape
    rank = left.shape[1]
    scale = 1.0 / math.sqrt(rank)
    size = cols // CHUNKS
    half = rows // 2
    part = half // PIECES
    blk = lax.axis_index("blk")
    lane = lax.axis_index("lane")
    ahead = lax.rem(blk + 1, blocks)
    behind = lax.rem(blk + blocks - 1, blocks)
    side = lax.rem(lane, 2)
    pair = lane + 1 - 2 * side
    peers = [lax.rem(lane + 2 * hop, lanes) for hop in range(1, lanes // 2)]

    loads = [
        pltpu.make_async_copy(left_hbm, left, load_sem.at[0]),
        pltpu.make_async_copy(right_hbm.at[0], visited.at[0], load_sem.at[1]),
    ]
    for s in range(steps):
        loads.append(pltpu.make_async_copy(obs_hbm.at[0, s], obs.at[s], load_sem.at[2 + s]))
    for copy in loads:
        copy.start()

    barrier = pltpu.get_barrier_semaphore()
    for neighbour in (behind, ahead):
        pl.semaphore_signal(barrier, inc=1, device_id={"blk": neighbour}, device_id_type=MESH)
    for friend in [pair] + peers:
        pl.semaphore_signal(barrier, inc=1, device_id={"lane": friend}, device_id_type=MESH)
    pl.semaphore_wait(barrier, 2 + 1 + len(peers))

    grad[...] = jnp.zeros_like(grad)
    loads[0].wait()
    loads[1].wait()

    def hop(s, k):
        span = pl.ds(pl.multiple_of(k * size, size), size)
        return pltpu.make_async_remote_copy(
            src_ref=updated.at[s, span],
            dst_ref=visited.at[s + 1, span],
            send_sem=send_sem.at[s, k],
            recv_sem=recv_sem.at[s, k],
            device_id={"blk": ahead},
            device_id_type=MESH,
        )

    def keep(k):
        span = pl.ds(pl.multiple_of(k * size, size), size)
        return pltpu.make_async_copy(updated.at[steps - 1, span], right_out.at[0, span], store_sem.at[k])

    for s in range(steps):
        loads[2 + s].wait()

        @pl.loop(0, CHUNKS)
        def _(k):
            span = pl.ds(pl.multiple_of(k * size, size), size)
            shifts = jnp.transpose(jnp.broadcast_to(shift_ref[s, pl.ds(k, 1), :], (size, size)))
            shifts = jnp.concatenate([shifts] * (rows // size), axis=1)
            seen = (jnp.right_shift(codes_ref[...], shifts) & 1) == 1
            if s > 0:
                hop(s - 1, k).wait_recv()
            block = visited[s, span, :]
            predicted = lax.dot_general(
                block, left[...], (((1,), (1,)), ((), ())), preferred_element_type=jnp.float32
            )
            error = predicted * scale - obs[s, span, :].astype(jnp.float32)
            error = jnp.where(seen, error, 0.0).astype(jnp.bfloat16)
            move = jnp.dot(error, left[...], preferred_element_type=jnp.float32)
            updated[s, span, :] = (block.astype(jnp.float32) - step_right * scale * move).astype(jnp.bfloat16)
            if s + 1 < steps:
                hop(s, k).start()
            else:
                keep(k).start()
            grad[...] += lax.dot_general(
                error, block, (((0,), (0,)), ((), ())), preferred_element_type=jnp.float32
            )

    mine = pl.multiple_of(side * half, half)
    other = pl.multiple_of((1 - side) * half, half)

    def swap(q):
        span = pl.ds(q * part, part)
        return pltpu.make_async_remote_copy(
            src_ref=pair_out.at[span], dst_ref=pair_in.at[span],
            send_sem=pair_send.at[q], recv_sem=pair_recv.at[q],
            device_id={"lane": pair}, device_id_type=MESH,
        )

    def cross(m, q):
        span = pl.ds(q * part, part)
        return pltpu.make_async_remote_copy(
            src_ref=peer_out.at[span], dst_ref=peer_in.at[m, span],
            send_sem=peer_send.at[m, q], recv_sem=peer_recv.at[m, q],
            device_id={"lane": peers[m]}, device_id_type=MESH,
        )

    def share(q):
        span = pl.ds(pl.multiple_of(mine + q * part, part), part)
        return pltpu.make_async_remote_copy(
            src_ref=result.at[span], dst_ref=result.at[span],
            send_sem=last_send.at[q], recv_sem=last_recv.at[q],
            device_id={"lane": pair}, device_id_type=MESH,
        )

    for q in range(PIECES):
        pair_out[pl.ds(q * part, part), :] = grad[pl.ds(pl.multiple_of(other + q * part, part), part), :].astype(jnp.bfloat16)
        swap(q).start()
    for q in range(PIECES):
        span = pl.ds(q * part, part)
        swap(q).wait_recv()
        peer_out[span, :] = (
            grad[pl.ds(pl.multiple_of(mine + q * part, part), part), :] + pair_in[span, :].astype(jnp.float32)
        ).astype(jnp.bfloat16)
        for m in range(len(peers)):
            cross(m, q).start()
    for q in range(PIECES):
        span = pl.ds(q * part, part)
        here = pl.ds(pl.multiple_of(mine + q * part, part), part)
        total = peer_out[span, :].astype(jnp.float32)
        for m in range(len(peers)):
            cross(m, q).wait_recv()
            total = total + peer_in[m, span, :].astype(jnp.float32)
        result[here, :] = (left[here, :].astype(jnp.float32) - step_left * scale * total).astype(jnp.bfloat16)
        share(q).start()
    own = pltpu.make_async_copy(result.at[pl.ds(mine, half)], left_out.at[pl.ds(mine, half)], out_sem.at[0])
    own.start()
    for q in range(PIECES):
        share(q).wait_recv()
    theirs = pltpu.make_async_copy(result.at[pl.ds(other, half)], left_out.at[pl.ds(other, half)], out_sem.at[1])
    theirs.start()
    for s in range(steps - 1):
        @pl.loop(0, CHUNKS)
        def _(k):
            hop(s, k).wait_send()

    @pl.loop(0, CHUNKS)
    def _(k):
        keep(k).wait()

    for q in range(PIECES):
        swap(q).wait_send()
        for m in range(len(peers)):
            cross(m, q).wait_send()
        share(q).wait_send()
    own.wait()
    theirs.wait()


def solution(mesh):
    blocks = mesh.shape["blk"]
    lanes = mesh.shape["lane"]

    def local(left_factor, right_factor, observed, row_codes, shift_codes):
        rows, rank = left_factor.shape
        _, steps, cols, _ = observed.shape
        size = cols // CHUNKS
        bf16, f32 = jnp.bfloat16, jnp.float32
        dma = pltpu.SemaphoreType.DMA
        anywhere = pl.BlockSpec(memory_space=pl.ANY)
        vmem = pl.BlockSpec(memory_space=pltpu.VMEM)
        others = lanes // 2 - 1
        return pl.pallas_call(
            functools.partial(kernel, blocks, lanes),
            out_shape=(
                jax.ShapeDtypeStruct((rows, rank), bf16),
                jax.ShapeDtypeStruct((1, cols, rank), bf16),
            ),
            in_specs=[anywhere, anywhere, anywhere, vmem, vmem],
            out_specs=(anywhere, anywhere),
            scratch_shapes=[
                pltpu.VMEM((rows, rank), bf16),
                pltpu.VMEM((steps, cols, rank), bf16),
                pltpu.VMEM((steps, cols, rank), bf16),
                pltpu.VMEM((steps, cols, rows), bf16),
                pltpu.VMEM((rows, rank), f32),
                pltpu.VMEM((rows // 2, rank), bf16),
                pltpu.VMEM((rows // 2, rank), bf16),
                pltpu.VMEM((rows // 2, rank), bf16),
                pltpu.VMEM((others, rows // 2, rank), bf16),
                pltpu.VMEM((rows, rank), bf16),
                dma((2 + steps,)),
                dma((steps - 1, CHUNKS)),
                dma((steps - 1, CHUNKS)),
                dma((CHUNKS,)),
                dma((PIECES,)),
                dma((PIECES,)),
                dma((others, PIECES)),
                dma((others, PIECES)),
                dma((PIECES,)),
                dma((PIECES,)),
                dma((2,)),
            ],
            compiler_params=pltpu.CompilerParams(
                collective_id=0, has_side_effects=True, vmem_limit_bytes=48 * 1024 * 1024
            ),
        )(
            left_factor, right_factor, observed,
            row_codes.reshape(1, rows), shift_codes.reshape(steps, CHUNKS, size),
        )

    in_specs = (
        P("blk", None),
        P("lane", "blk", None),
        P("lane", None, None, "blk"),
        P("blk"),
        P("lane", None, "blk"),
    )
    out_specs = (P("blk", None), P("lane", "blk", None))
    return jax.shard_map(local, mesh=mesh, in_specs=in_specs, out_specs=out_specs, check_vma=False)
```

time: 94.3 us -> 60.5 us (0.64)
  waiting for transfers between devices: 61.1 us -> 0 us
  Pallas kernels: 0 us -> 52.9 us
  between operations: 14.3 us -> 0.64 us
  matrix products: 10.2 us -> 0 us
  local copies, waits for them, and re-layouts: 0.95 us -> 6.65 us
  starting transfers between devices: 4.89 us -> 0 us
  other arithmetic: 2.82 us -> 0 us
    pallas_call x0 -> x1, Pallas kernels: none -> 52.9 us  [local(): pl.pallas_call(functools.partial(kernel, blocks, lanes), out_shape=(jax.S...]
    ppermute x6 -> x0, waiting for transfers between devices: 30.7 us -> none  [passed_along(): return lax.ppermute(value, axis, pairs)]
    psum x1 -> x0, waiting for transfers between devices: 30.3 us -> none  [local(): summed = lax.psum(grad_sum.astype(jnp.bfloat16), 'lane').astype(jnp.float32)]
    dot_general x24 -> x0, matrix products: 10.2 us -> none  [the longest x8 4.16 us: visit_tile(): lax.dot_general(right_part, left_factor, (((1,), (1,)), ((), ())), prefer...]
    unnamed x8 -> x10, local copies, waits for them, and re-layouts: 0.03 us -> 5.94 us
    ppermute x6 -> x0, starting transfers between devices: 4.85 us -> none  [passed_along(): return lax.ppermute(value, axis, pairs)]
    convert_element_type x1 -> x0, other arithmetic: 1.99 us -> none  [local(): (left_factor.astype(jnp.float32) - step_left * root_scale * summed).astyp...]
  transfers between devices with their start and end apart: 7 -> 0, of which waited for: 6 -> 0; matrix products, arithmetic and copies ran while one was open for 8% -> 0% of each run, Pallas kernels for 0% -> 0%
where the time goes in v1:
time: 60.5 us; the launch traced here: 60.2 us
  Pallas kernels  52.9 us (87%)
  local copies, waits for them, and re-layouts  6.65 us (11%)
  between operations  0.64 us (1%)
    pallas_call x1, Pallas kernels, local(): pl.pallas_call(functools.partial(kernel, blocks, lanes), out_shape=(jax.S...  52.9 us
    unnamed x10, local copies, waits for them, and re-layouts  5.94 us

profile of v1, /device:TPU:0, one launch (start us, length us, event | category | flops | bytes accessed | tf_op | source)
XLA Modules:
  0.0 60.2 jit_solution(2018192751713905370)
XLA Ops:
  0.6 0.7 %reshape.11.shift_ref = s32[4,4,128]{2,1,0:T(4,128)S(1)} reshape(s32[1,4,512]{2,1,0:T(4,128)} %param.9) | data formatting | bytes 16384 | tf_op jit(solution)/shard_map/reshape | solution.py:222
  1.3 0.0 copy-start
  1.3 1.6 %copy-done = bf16[1,4,512,512]{3,2,1,0:T(8,128)(2,1)S(1)} copy-done((bf16[1,4,512,512]{3,2,1,0:T(8,128)(2,1)S(1)}, bf16[1,4,512,512]{3,2,1,0:T(8,128)(2,1)}, u32[]{:S(2)}) %copy-start) | copy-done | bytes 2097176
  2.9 0.0 copy-start.1
  2.9 1.0 %copy-done.1 = bf16[512,512]{1,0:T(8,128)(2,1)S(1)} copy-done((bf16[512,512]{1,0:T(8,128)(2,1)S(1)}, bf16[512,512]{1,0:T(8,128)(2,1)}, u32[]{:S(2)}) %copy-start.1) | copy-done | bytes 524312
  4.0 0.0 copy-start.2
  4.0 1.0 %copy-done.2 = bf16[1,512,512]{2,1,0:T(8,128)(2,1)S(1)} copy-done((bf16[1,512,512]{2,1,0:T(8,128)(2,1)S(1)}, bf16[1,512,512]{2,1,0:T(8,128)(2,1)}, u32[]{:S(2)}) %copy-start.2) | copy-done | bytes 524312
  5.0 0.0 copy-start.3
  5.0 0.7 %copy-done.3 = s32[512]{0:T(512)S(1)} copy-done((s32[512]{0:T(512)S(1)}, s32[512]{0:T(512)}, u32[]{:S(2)}) %copy-start.3) | copy-done | bytes 2072
  5.7 52.9 %shard_map.68 = (bf16[512,512]{1,0:T(8,128)(2,1)S(1)}, bf16[1,512,512]{2,1,0:T(8,128)(2,1)S(1)}) custom-call(bf16[512,512]{1,0:T(8,128)(2,1)S(1)} %copy-done.1, bf16[1,512,512]{2,1,0:T(8,128)(2,1)S(1)} %copy-done.2, bf16[1,4,512,512]{3,2,1,0:T(8,128)(2,1)S(1)} %copy-done, s32[1,512]{1,0:T(1,128)S(1)} %bitcast.1, s32[4,4,128]{2,1,0:T(4,128)S(1)} %reshape.11.shift_ref), custom_call_target="tpu_custom_call" | custom-call | tf_op jit(solution)/shard_map/pallas_call | solution.py:186
  58.6 0.8 %copy.9 = bf16[512,512]{1,0:T(8,128)(2,1)} copy(bf16[512,512]{1,0:T(8,128)(2,1)S(1)} %get-tuple-element.4) | data formatting | bytes 1048576
  59.4 0.8 %copy.10 = bf16[1,512,512]{2,1,0:T(8,128)(2,1)} copy(bf16[1,512,512]{2,1,0:T(8,128)(2,1)S(1)} %get-tuple-element.5) | data formatting | bytes 1048576
Async XLA Ops:
  1.3 1.6 %copy-start = (bf16[1,4,512,512]{3,2,1,0:T(8,128)(2,1)S(1)}, bf16[1,4,512,512]{3,2,1,0:T(8,128)(2,1)}, u32[]{:S(2)}) copy-start(bf16[1,4,512,512]{3,2,1,0:T(8,128)(2,1)} %obs_hbm.1) | copy-start | bytes 6291460
  2.9 1.0 %copy-start.1 = (bf16[512,512]{1,0:T(8,128)(2,1)S(1)}, bf16[512,512]{1,0:T(8,128)(2,1)}, u32[]{:S(2)}) copy-start(bf16[512,512]{1,0:T(8,128)(2,1)} %left_hbm.1) | copy-start | bytes 1572868
  4.0 1.0 %copy-start.2 = (bf16[1,512,512]{2,1,0:T(8,128)(2,1)S(1)}, bf16[1,512,512]{2,1,0:T(8,128)(2,1)}, u32[]{:S(2)}) copy-start(bf16[1,512,512]{2,1,0:T(8,128)(2,1)} %right_hbm.1) | copy-start | bytes 1572868
  5.0 0.7 %copy-start.3 = (s32[512]{0:T(512)S(1)}, s32[512]{0:T(512)}, u32[]{:S(2)}) copy-start(s32[512]{0:T(512)} %param.8) | copy-start | bytes 6148

commit v2 on v1

--- a/solution.py
+++ b/solution.py
@@ -78,7 +78,7 @@
         @pl.loop(0, CHUNKS)
         def _(k):
             span = pl.ds(pl.multiple_of(k * size, size), size)
-            shifts = jnp.transpose(jnp.broadcast_to(shift_ref[s, pl.ds(k, 1), :], (size, size)))
+            shifts = jnp.transpose(jnp.broadcast_to(shift_ref[0, pl.ds(s, 1), span], (size, size)))
             shifts = jnp.concatenate([shifts] * (rows // size), axis=1)
             seen = (jnp.right_shift(codes_ref[...], shifts) & 1) == 1
             if s > 0:
@@ -215,11 +215,11 @@
                 dma((2,)),
             ],
             compiler_params=pltpu.CompilerParams(
-                collective_id=0, has_side_effects=True, vmem_limit_bytes=48 * 1024 * 1024
+                collective_id=0, has_side_effects=True, vmem_limit_bytes=67043328
             ),
         )(
             left_factor, right_factor, observed,
-            row_codes.reshape(1, rows), shift_codes.reshape(steps, CHUNKS, size),
+            row_codes.reshape(1, rows), shift_codes,
         )
 
     in_specs = (

time: 60.5 us -> 58.8 us (0.972)
  local copies, waits for them, and re-layouts: 6.65 us -> 3.74 us
  Pallas kernels: 52.9 us -> 54.1 us
    unnamed x10 -> x2, local copies, waits for them, and re-layouts: 5.94 us -> 3.74 us
    pallas_call x1, Pallas kernels: 52.9 us -> 54.1 us  [local(): pl.pallas_call(functools.partial(kernel, blocks, lanes), out_shape=(jax.S...]
    reshape x1 -> x0, local copies, waits for them, and re-layouts: 0.71 us -> none  [local(): shift_codes.reshape(steps, CHUNKS, size)]
where the time goes in v2:
time: 58.8 us; the launch traced here: 58.5 us
  Pallas kernels  54.1 us (92%)
  local copies, waits for them, and re-layouts  3.74 us (6%)
  between operations  0.64 us (1%)
    pallas_call x1, Pallas kernels, local(): pl.pallas_call(functools.partial(kernel, blocks, lanes), out_shape=(jax.S...  54.1 us
    unnamed x2, local copies, waits for them, and re-layouts  3.74 us

profile of v2, /device:TPU:0, one launch (start us, length us, event | category | flops | bytes accessed | tf_op | source)
XLA Modules:
  0.0 58.5 jit_solution(10368266636267613756)
XLA Ops:
  0.6 54.1 %shard_map.68 = (bf16[512,512]{1,0:T(8,128)(2,1)}, bf16[1,512,512]{2,1,0:T(8,128)(2,1)}) custom-call(bf16[512,512]{1,0:T(8,128)(2,1)} %left_hbm.1, bf16[1,512,512]{2,1,0:T(8,128)(2,1)} %right_hbm.1, bf16[1,4,512,512]{3,2,1,0:T(8,128)(2,1)} %obs_hbm.1, s32[1,512]{1,0:T(1,128)} %bitcast.1, s32[1,4,512]{2,1,0:T(4,128)} %shift_ref.1), custom_call_target="tpu_custom_call" | custom-call | tf_op jit(solution)/shard_map/pallas_call | solution.py:186
  54.8 1.9 %copy.9 = bf16[512,512]{1,0:T(8,128)(2,1)} copy(bf16[512,512]{1,0:T(8,128)(2,1)} %get-tuple-element.4) | data formatting | bytes 1048576
  56.6 1.9 %copy.10 = bf16[1,512,512]{2,1,0:T(8,128)(2,1)} copy(bf16[1,512,512]{2,1,0:T(8,128)(2,1)} %get-tuple-element.5) | data formatting | bytes 1048576

commit v3 on v2

v3 whole, which is shorter than its diff:
```python
import functools
import math

import jax
import jax.numpy as jnp
from jax import lax
from jax.experimental import pallas as pl
from jax.experimental.pallas import tpu as pltpu
from jax.sharding import PartitionSpec as P

step_right = 0.25
step_left = 0.1

CHUNKS = 4
WIDTH = 128
PARTS = 2
PIECES = 4
MESH = pl.DeviceIdType.MESH


def kernel(
    blocks, lanes,
    left_hbm, right_hbm, obs_hbm, codes_hbm, shift_hbm,
    left_out, right_out,
    left, visited, updated, obs, codes, shift, turned, errors, grad, pair_out, pair_in, peer_out, peer_in, result,
    load_sem, send_sem, recv_sem, pair_send, pair_recv, peer_send, peer_recv, last_send, last_recv, out_sem,
):
    steps, cols, rows = obs.shape
    rank = left.shape[1]
    scale = 1.0 / math.sqrt(rank)
    size = cols // CHUNKS
    half = rows // 2
    part = half // PIECES
    width = turned.shape[1]
    blk = lax.axis_index("blk")
    lane = lax.axis_index("lane")
    ahead = lax.rem(blk + 1, blocks)
    behind = lax.rem(blk + blocks - 1, blocks)
    side = lax.rem(lane, 2)
    pair = lane + 1 - 2 * side
    peers = [lax.rem(lane + 2 * hop, lanes) for hop in range(1, lanes // 2)]
    mine = pl.multiple_of(side * half, half)
    other = pl.multiple_of((1 - side) * half, half)

    barrier = pltpu.get_barrier_semaphore()
    for neighbour in (behind, ahead):
        pl.semaphore_signal(barrier, inc=1, device_id={"blk": neighbour}, device_id_type=MESH)
    for friend in [pair] + peers:
        pl.semaphore_signal(barrier, inc=1, device_id={"lane": friend}, device_id_type=MESH)

    loads = [
        pltpu.make_async_copy(shift_hbm, shift, load_sem.at[0]),
        pltpu.make_async_copy(codes_hbm, codes, load_sem.at[1]),
        pltpu.make_async_copy(right_hbm.at[0], visited.at[0], load_sem.at[2]),
        pltpu.make_async_copy(left_hbm, left, load_sem.at[3]),
    ]
    for s in range(steps):
        loads.append(pltpu.make_async_copy(obs_hbm.at[0, s], obs.at[s], load_sem.at[4 + s]))
    for copy in loads:
        copy.start()

    def hop(s, k):
        span = pl.ds(pl.multiple_of(k * size, size), size)
        return pltpu.make_async_remote_copy(
            src_ref=updated.at[s, span],
            dst_ref=visited.at[s + 1, span],
            send_sem=send_sem.at[s, k],
            recv_sem=recv_sem.at[s, k],
            device_id={"blk": ahead},
            device_id_type=MESH,
        )

    def turn(s):
        for first in range(0, cols, width):
            span = pl.ds(first, width)
            turned[span, :] = jnp.transpose(jnp.broadcast_to(shift[0, pl.ds(s, 1), span], (width, width)))

    def error_of(s, k):
        span = pl.ds(pl.multiple_of(k * size, size), size)
        shifts = jnp.concatenate([turned[span, :]] * (rows // width), axis=1)
        seen = (jnp.right_shift(codes[...], shifts) & 1) == 1
        predicted = lax.dot_general(
            visited[s, span, :], left[...], (((1,), (1,)), ((), ())), preferred_element_type=jnp.float32
        )
        error = predicted * scale - obs[s, span, :].astype(jnp.float32)
        return jnp.where(seen, error, 0.0).astype(jnp.bfloat16)

    def stepped(error, block):
        move = jnp.dot(error, left[...], preferred_element_type=jnp.float32)
        return (block.astype(jnp.float32) - step_right * scale * move).astype(jnp.bfloat16)

    def add_left(error, block):
        grad[...] += lax.dot_general(
            error, block, (((0,), (0,)), ((), ())), preferred_element_type=jnp.float32
        )

    def visit(s, k, before_send=None):
        span = pl.ds(pl.multiple_of(k * size, size), size)
        if s > 0:
            hop(s - 1, k).wait_recv()
        error = error_of(s, k)
        block = visited[s, span, :]
        updated[s, span, :] = stepped(error, block)
        if before_send is not None:
            before_send()
        hop(s, k).start()
        add_left(error, block)

    loads[0].wait()
    turn(0)
    grad[...] = jnp.zeros_like(grad)
    for copy in loads[1:5]:
        copy.wait()
    visit(0, 0, lambda: pl.semaphore_wait(barrier, 2 + 1 + len(peers)))
    for s in range(steps - 1):
        if s > 0:
            loads[4 + s].wait()
            turn(s)
        pl.loop(1 if s == 0 else 0, CHUNKS)(functools.partial(visit, s))

    last = steps - 1
    loads[4 + last].wait()
    turn(last)

    @pl.loop(0, CHUNKS - 1)
    def _(k):
        span = pl.ds(pl.multiple_of(k * size, size), size)
        hop(last - 1, k).wait_recv()
        error = error_of(last, k)
        errors[span, :] = error
        add_left(error, visited[last, span, :])

    tail = pl.ds((CHUNKS - 1) * size, size)
    hop(last - 1, CHUNKS - 1).wait_recv()
    errors[tail, :] = error_of(last, CHUNKS - 1)

    def finish(first):
        span = pl.ds(first, half)
        return grad[span, :] + lax.dot_general(
            errors[tail, span], visited[last, tail, :], (((0,), (0,)), ((), ())), preferred_element_type=jnp.float32
        )

    def swap(q):
        span = pl.ds(q * part, part)
        return pltpu.make_async_remote_copy(
            src_ref=pair_out.at[span], dst_ref=pair_in.at[span],
            send_sem=pair_send.at[q], recv_sem=pair_recv.at[q],
            device_id={"lane": pair}, device_id_type=MESH,
        )

    def cross(m, q):
        span = pl.ds(q * part, part)
        return pltpu.make_async_remote_copy(
            src_ref=peer_out.at[span], dst_ref=peer_in.at[m, span],
            send_sem=peer_send.at[m, q], recv_sem=peer_recv.at[m, q],
            device_id={"lane": peers[m]}, device_id_type=MESH,
        )

    def share(q):
        span = pl.ds(pl.multiple_of(mine + q * part, part), part)
        return pltpu.make_async_remote_copy(
            src_ref=result.at[span], dst_ref=result.at[span],
            send_sem=last_send.at[q], recv_sem=last_recv.at[q],
            device_id={"lane": pair}, device_id_type=MESH,
        )

    pair_out[...] = finish(other).astype(jnp.bfloat16)
    for q in range(PIECES):
        swap(q).start()
    grad[pl.ds(mine, half), :] = finish(mine)
    for q in range(PIECES):
        span = pl.ds(q * part, part)
        swap(q).wait_recv()
        peer_out[span, :] = (
            grad[pl.ds(pl.multiple_of(mine + q * part, part), part), :] + pair_in[span, :].astype(jnp.float32)
        ).astype(jnp.bfloat16)
        for m in range(len(peers)):
            cross(m, q).start()

    @pl.loop(0, CHUNKS)
    def _(k):
        span = pl.ds(pl.multiple_of(k * size, size), size)
        updated[last, span, :] = stepped(errors[span, :], visited[last, span, :])

    outs = [
        pltpu.make_async_copy(updated.at[last], right_out.at[0], out_sem.at[0]),
        pltpu.make_async_copy(result.at[pl.ds(mine, half)], left_out.at[pl.ds(mine, half)], out_sem.at[1]),
        pltpu.make_async_copy(result.at[pl.ds(other, half)], left_out.at[pl.ds(other, half)], out_sem.at[2]),
    ]
    outs[0].start()
    for s in range(steps - 1):
        @pl.loop(0, CHUNKS)
        def _(k):
            hop(s, k).wait_send()

    for q in range(PIECES):
        span = pl.ds(q * part, part)
        here = pl.ds(pl.multiple_of(mine + q * part, part), part)
        total = peer_out[span, :].astype(jnp.float32)
        for m in range(len(peers)):
            cross(m, q).wait_recv()
            total = total + peer_in[m, span, :].astype(jnp.float32)
        result[here, :] = (left[here, :].astype(jnp.float32) - step_left * scale * total).astype(jnp.bfloat16)
        share(q).start()
    outs[1].start()
    for q in range(PIECES):
        share(q).wait_recv()
    outs[2].start()
    for q in range(PIECES):
        swap(q).wait_send()
        for m in range(len(peers)):
            cross(m, q).wait_send()
        share(q).wait_send()
    for copy in outs:
        copy.wait()


def place(left_from, right_from, left_to, right_to, held, in_sem, out_sem):
    pairs = [(left_from, left_to), (right_from.at[0], right_to.at[0])]
    rows = left_from.shape[0] // PARTS
    moves = []
    for which, (source, target) in enumerate(pairs):
        for p in range(PARTS):
            span = pl.ds(p * rows, rows)
            moves.append((
                pltpu.make_async_copy(source.at[span], held.at[which, span], in_sem.at[which, p]),
                pltpu.make_async_copy(held.at[which, span], target.at[span], out_sem.at[which, p]),
            ))
    for inward, _ in moves:
        inward.start()
    for inward, outward in moves:
        inward.wait()
        outward.start()
    for _, outward in moves:
        outward.wait()


def solution(mesh):
    blocks = mesh.shape["blk"]
    lanes = mesh.shape["lane"]

    def local(left_factor, right_factor, observed, row_codes, shift_codes):
        rows, rank = left_factor.shape
        _, steps, cols, _ = observed.shape
        bf16, f32 = jnp.bfloat16, jnp.float32
        dma = pltpu.SemaphoreType.DMA
        hbm = pl.BlockSpec(memory_space=pltpu.HBM)
        others = lanes // 2 - 1
        shapes = (
            jax.ShapeDtypeStruct((rows, rank), bf16),
            jax.ShapeDtypeStruct((1, cols, rank), bf16),
        )
        results = pl.pallas_call(
            functools.partial(kernel, blocks, lanes),
            out_shape=shapes,
            in_specs=[hbm] * 5,
            out_specs=(hbm, hbm),
            scratch_shapes=[
                pltpu.VMEM((rows, rank), bf16),
                pltpu.VMEM((steps, cols, rank), bf16),
                pltpu.VMEM((steps, cols, rank), bf16),
                pltpu.VMEM((steps, cols, rows), bf16),
                pltpu.VMEM((1, rows), jnp.int32),
                pltpu.VMEM((1, steps, cols), jnp.int32),
                pltpu.VMEM((cols, WIDTH), jnp.int32),
                pltpu.VMEM((cols, rows), bf16),
                pltpu.VMEM((rows, rank), f32),
                pltpu.VMEM((rows // 2, rank), bf16),
                pltpu.VMEM((rows // 2, rank), bf16),
                pltpu.VMEM((rows // 2, rank), bf16),
                pltpu.VMEM((others, rows // 2, rank), bf16),
                pltpu.VMEM((rows, rank), bf16),
                dma((4 + steps,)),
                dma((steps - 1, CHUNKS)),
                dma((steps - 1, CHUNKS)),
                dma((PIECES,)),
                dma((PIECES,)),
                dma((others, PIECES)),
                dma((others, PIECES)),
                dma((PIECES,)),
                dma((PIECES,)),
                dma((3,)),
            ],
            compiler_params=pltpu.CompilerParams(
                collective_id=0, has_side_effects=True, vmem_limit_bytes=67043328
            ),
        )(
            left_factor, right_factor, observed,
            row_codes.reshape(1, rows), shift_codes,
        )
        return pl.pallas_call(
            place,
            out_shape=shapes,
            in_specs=[hbm] * 2,
            out_specs=(hbm, hbm),
            scratch_shapes=[pltpu.VMEM((2, max(rows, cols), rank), bf16), dma((2, PARTS)), dma((2, PARTS))],
            compiler_params=pltpu.CompilerParams(vmem_limit_bytes=67043328),
        )(*results)

    in_specs = (
        P("blk", None),
        P("lane", "blk", None),
        P("lane", None, None, "blk"),
        P("blk"),
        P("lane", None, "blk"),
    )
    out_specs = (P("blk", None), P("lane", "blk", None))
    return jax.shard_map(local, mesh=mesh, in_specs=in_specs, out_specs=out_specs, check_vma=False)
```

time: 58.8 us -> 56.5 us (0.961)
  local copies, waits for them, and re-layouts: 3.74 us -> 0 us
  Pallas kernels: 54.1 us -> 55.7 us
    unnamed x2 -> x0, local copies, waits for them, and re-layouts: 3.74 us -> none
    pallas_call x1 -> x2, Pallas kernels: 54.1 us -> 55.7 us  [the longest x1 53.7 us: local(): pl.pallas_call(functools.partial(kernel, blocks, lanes), out_shape=shapes...]
where the time goes in v3:
time: 56.5 us; the launch traced here: 56.3 us
  Pallas kernels  55.7 us (99%)
  between operations  0.64 us (1%)
    pallas_call x1, Pallas kernels, local(): pl.pallas_call(functools.partial(kernel, blocks, lanes), out_shape=shapes...  53.7 us
    pallas_call x1, Pallas kernels, local(): pl.pallas_call(place, out_shape=shapes, in_specs=[hbm] * 2, out_specs=(hb...  1.98 us

profile of v3, /device:TPU:0, one launch (start us, length us, event | category | flops | bytes accessed | tf_op | source)
XLA Modules:
  0.0 56.3 jit_solution(11586586161646893400)
XLA Ops:
  0.6 53.7 %shard_map.68 = (bf16[512,512]{1,0:T(8,128)(2,1)}, bf16[1,512,512]{2,1,0:T(8,128)(2,1)}) custom-call(bf16[512,512]{1,0:T(8,128)(2,1)} %left_hbm.1, bf16[1,512,512]{2,1,0:T(8,128)(2,1)} %right_hbm.1, bf16[1,4,512,512]{3,2,1,0:T(8,128)(2,1)} %obs_hbm.1, s32[1,512]{1,0:T(1,128)} %bitcast.1, s32[1,4,512]{2,1,0:T(4,128)} %shift_hbm.1), custom_call_target="tpu_custom_call" | custom-call | tf_op jit(solution)/shard_map/pallas_call | solution.py:253
  54.3 2.0 %shard_map.69 = (bf16[512,512]{1,0:T(8,128)(2,1)}, bf16[1,512,512]{2,1,0:T(8,128)(2,1)}) custom-call(bf16[512,512]{1,0:T(8,128)(2,1)} %get-tuple-element.4.left_from, bf16[1,512,512]{2,1,0:T(8,128)(2,1)} %get-tuple-element.5.right_from), custom_call_target="tpu_custom_call" | custom-call | tf_op jit(solution)/shard_map/pallas_call | solution.py:291

commit v4 on v3

--- a/solution.py
+++ b/solution.py
@@ -43,8 +43,7 @@
     other = pl.multiple_of((1 - side) * half, half)
 
     barrier = pltpu.get_barrier_semaphore()
-    for neighbour in (behind, ahead):
-        pl.semaphore_signal(barrier, inc=1, device_id={"blk": neighbour}, device_id_type=MESH)
+    pl.semaphore_signal(barrier, inc=1, device_id={"blk": behind}, device_id_type=MESH)
     for friend in [pair] + peers:
         pl.semaphore_signal(barrier, inc=1, device_id={"lane": friend}, device_id_type=MESH)
 
@@ -56,7 +55,7 @@
     ]
     for s in range(steps):
         loads.append(pltpu.make_async_copy(obs_hbm.at[0, s], obs.at[s], load_sem.at[4 + s]))
-    for copy in loads:
+    for copy in loads[:5]:
         copy.start()
 
     def hop(s, k):
@@ -106,12 +105,14 @@
         hop(s, k).start()
         add_left(error, block)
 
+    grad[...] = jnp.zeros_like(grad)
     loads[0].wait()
     turn(0)
-    grad[...] = jnp.zeros_like(grad)
     for copy in loads[1:5]:
         copy.wait()
-    visit(0, 0, lambda: pl.semaphore_wait(barrier, 2 + 1 + len(peers)))
+    visit(0, 0, lambda: pl.semaphore_wait(barrier, 2 + len(peers)))
+    for copy in loads[5:]:
+        copy.start()
     for s in range(steps - 1):
         if s > 0:
             loads[4 + s].wait()

time: 56.5 us -> 56.5 us (level)
  no operation moved by 1% of the time
where the time goes in v4:
time: 56.5 us; the launch traced here: 56.3 us
  Pallas kernels  55.7 us (99%)
  between operations  0.64 us (1%)
    pallas_call x1, Pallas kernels, local(): pl.pallas_call(functools.partial(kernel, blocks, lanes), out_shape=shapes...  53.7 us
    pallas_call x1, Pallas kernels, local(): pl.pallas_call(place, out_shape=shapes, in_specs=[hbm] * 2, out_specs=(hb...  1.98 us

profile of v4, /device:TPU:0, one launch (start us, length us, event | category | flops | bytes accessed | tf_op | source)
XLA Modules:
  0.0 56.3 jit_solution(16462920265520179514)
XLA Ops:
  0.6 53.7 %shard_map.68 = (bf16[512,512]{1,0:T(8,128)(2,1)}, bf16[1,512,512]{2,1,0:T(8,128)(2,1)}) custom-call(bf16[512,512]{1,0:T(8,128)(2,1)} %left_hbm.1, bf16[1,512,512]{2,1,0:T(8,128)(2,1)} %right_hbm.1, bf16[1,4,512,512]{3,2,1,0:T(8,128)(2,1)} %obs_hbm.1, s32[1,512]{1,0:T(1,128)} %bitcast.1, s32[1,4,512]{2,1,0:T(4,128)} %shift_hbm.1), custom_call_target="tpu_custom_call" | custom-call | tf_op jit(solution)/shard_map/pallas_call | solution.py:254
  54.3 2.0 %shard_map.69 = (bf16[512,512]{1,0:T(8,128)(2,1)}, bf16[1,512,512]{2,1,0:T(8,128)(2,1)}) custom-call(bf16[512,512]{1,0:T(8,128)(2,1)} %get-tuple-element.4.left_from, bf16[1,512,512]{2,1,0:T(8,128)(2,1)} %get-tuple-element.5.right_from), custom_call_target="tpu_custom_call" | custom-call | tf_op jit(solution)/shard_map/pallas_call | solution.py:292
